TPU v7x, 32 devices: a whole 2x2x4 slice. The times are simulated.
32 devices in a mesh: grp: 16 (over z, y, core), tp: 2 (over x).
Axes of the slice: x: 2, y: 2, z: 4, core: 2. Of those that a mesh axis runs over, the one named last changes fastest.
Arguments:
- tokens: bfloat16 [1024, 6144], P('grp', 'tp'), may hold values from -6 to 6
- norm_gain: float32 [6144], replicated, may hold values from 0.25 to 1.75
- router_weight: bfloat16 [6144, 8], replicated, may hold values from -0.078125 to 0.078125
- expert_ids: int32 [1024, 2], P('grp'), may hold values from 0 to 7, all different within a row; in each aligned block of 64 rows (0 to 63, 64 to 127, ...) at most 18 rows name the same one
- gate_proj: bfloat16 [6144, 65536], P(None, ('grp', 'tp')), may hold values from -0.078125 to 0.078125
- up_proj: bfloat16 [6144, 65536], P(None, ('grp', 'tp')), may hold values from -0.078125 to 0.078125
- down_proj: bfloat16 [65536, 6144], P(('grp', 'tp')), may hold values from -0.125 to 0.125
Outputs:
- mixed: bfloat16 [1024, 6144], P('grp', 'tp')
Inputs may be any that keep to these rules, and one draw needn't show every extreme that they name: `expert_ids`: each row names two different experts; within the rows of one group (aligned blocks of 64 rows) no expert is named more than 18 times, and in some group one expert is named exactly 18 times.
All inputs are finite; a program needn't handle non-finite values.
Results may differ from a plain program's by a relative error of at most 0.017.
Values may be sent and summed in bfloat16 or wider, within the bound.
A program may use at most 128 MiB of HBM per device.

v0:
```python
from functools import partial

import jax
import jax.numpy as jnp
from jax import lax
from jax.experimental import pallas as pl
from jax.experimental.pallas import tpu as pltpu
from jax.sharding import PartitionSpec as P

CAP = 18
MESH = pl.DeviceIdType.MESH


epsilon = 1e-05


def place(experts, owners, pieces):
    g, p = lax.axis_index("grp"), lax.axis_index("tp")
    return g, p, g // owners, lax.rem(g, owners)


def greet(experts, owners, pieces):
    g, p, c, k = place(experts, owners, pieces)
    barrier = pltpu.get_barrier_semaphore()
    peers = [(lax.rem(c + j, experts) * owners + k, p) for j in range(1, experts)]
    peers += [(c * owners + lax.rem(k + d, owners), p) for d in range(1, owners)]
    peers += [(g, lax.rem(p + t, pieces)) for t in range(1, pieces)]
    for peer in peers:
        pl.semaphore_signal(barrier, inc=1, device_id=peer, device_id_type=MESH)
    pl.semaphore_wait(barrier, len(peers))


def remote(src, dst, sems, index, peer):
    return pltpu.make_async_remote_copy(
        src_ref=src,
        dst_ref=dst,
        send_sem=sems.at[(0,) + index],
        recv_sem=sems.at[(1,) + index],
        device_id=peer,
        device_id_type=MESH,
    )


def slabs_of(experts, owners, pieces, capacity, width):
    for t in range(pieces):
        for s in range(experts):
            for o in range(owners):
                rows = pl.ds((s * owners + o) * capacity, capacity)
                yield (t, s, o), (rows, pl.ds(t * width, width))


def dispatch_kernel(
    experts, owners, pieces, src, rows_out, out, local, direct, core, cross, cross_core
):
    g, p, c, k = place(experts, owners, pieces)
    greet(experts, owners, pieces)
    keep = pltpu.make_async_copy(src.at[c], out.at[p, c, k], local)
    keep.start()
    sends = {}
    for j in range(1, experts):
        e = lax.rem(c + j, experts)
        sends[j] = remote(src.at[e], out.at[p, c, k], direct, (j,), (e * owners + k, p))
        sends[j].start()
    to_core, to_piece, to_cross = [], {}, []
    for j in range(experts):
        s = lax.rem(c + experts - j, experts)
        if j == 0:
            keep.wait()
        else:
            sends[j].wait_recv()
        slab = out.at[p, s, k]
        for t in range(1, pieces):
            copy = remote(slab, slab, cross, (t, j), (g, lax.rem(p + t, pieces)))
            copy.start()
            to_piece[t, j] = copy
        for d in range(1, owners):
            peer = (c * owners + lax.rem(k + d, owners), p)
            copy = remote(slab, slab, core, (d, j), peer)
            copy.start()
            to_core.append(copy)
    for j in range(experts):
        s = lax.rem(c + experts - j, experts)
        for t in range(1, pieces):
            to_piece[t, j].wait_recv()
            slab = out.at[lax.rem(p + pieces - t, pieces), s, k]
            for d in range(1, owners):
                peer = (c * owners + lax.rem(k + d, owners), p)
                copy = remote(slab, slab, cross_core, (t, d, j), peer)
                copy.start()
                to_cross.append(copy)
    for copy in to_core + to_cross:
        copy.wait()
    for copy in list(sends.values()) + list(to_piece.values()):
        copy.wait_send()
    for slab, block in slabs_of(experts, owners, pieces, *src.shape[1:]):
        rows_out[block] = out[slab]


def collect_kernel(
    experts, owners, pieces, rows_in, out, part, near, leaving, arrived, final, core, cross, back
):
    g, p, c, k = place(experts, owners, pieces)
    greet(experts, owners, pieces)
    order = list(range(1, experts)) + [0]
    near_copies, cross_copies, back_copies = {}, {}, {}
    for slab, block in slabs_of(experts, owners, pieces, *out.shape[1:]):
        part[slab] = rows_in[block]
    for t in list(range(1, pieces)) + [0]:
        for j in order:
            s = lax.rem(c + j, experts)
            piece = lax.rem(p + t, pieces)
            for d in range(1, owners):
                other = lax.rem(k + d, owners)
                copy = remote(
                    part.at[piece, s, other],
                    near.at[d - 1, t, j],
                    core,
                    (d, t, j),
                    (c * owners + other, p),
                )
                copy.start()
                near_copies[d, t, j] = copy

    def chip_sum(t, j):
        total = part[lax.rem(p + t, pieces), lax.rem(c + j, experts), k].astype(jnp.float32)
        for d in range(1, owners):
            near_copies[d, t, j].wait_recv()
            total = total + near[d - 1, t, j].astype(jnp.float32)
        return total

    for j in order:
        for t in range(1, pieces):
            leaving[t - 1, j] = chip_sum(t, j).astype(leaving.dtype)
            copy = remote(
                leaving.at[t - 1, j],
                arrived.at[t - 1, j],
                cross,
                (t, j),
                (g, lax.rem(p + t, pieces)),
            )
            copy.start()
            cross_copies[t, j] = copy
    for j in order:
        total = chip_sum(0, j)
        for t in range(1, pieces):
            cross_copies[t, j].wait_recv()
            total = total + arrived[t - 1, j].astype(jnp.float32)
        if j == 0:
            out[c] = total.astype(out.dtype)
        else:
            final[j] = total.astype(final.dtype)
            peer = (lax.rem(c + j, experts) * owners + k, p)
            copy = remote(final.at[j], out.at[c], back, (j,), peer)
            copy.start()
            back_copies[j] = copy
    for copy in back_copies.values():
        copy.wait()
    for copy in list(near_copies.values()) + list(cross_copies.values()):
        copy.wait_send()


def dispatch(outgoing, owners, pieces):
    experts, capacity, width = outgoing.shape
    dma = pltpu.SemaphoreType.DMA
    return pl.pallas_call(
        partial(dispatch_kernel, experts, owners, pieces),
        out_shape=jax.ShapeDtypeStruct(
            (experts * owners * capacity, pieces * width), outgoing.dtype
        ),
        in_specs=[pl.BlockSpec(memory_space=pltpu.VMEM)],
        out_specs=pl.BlockSpec(memory_space=pltpu.VMEM),
        scratch_shapes=[
            pltpu.VMEM((pieces, experts, owners, capacity, width), outgoing.dtype),
            dma,
            dma((2, experts)),
            dma((2, owners, experts)),
            dma((2, pieces, experts)),
            dma((2, pieces, owners, experts)),
        ],
        compiler_params=pltpu.CompilerParams(
            collective_id=0, has_side_effects=True, vmem_limit_bytes=60 * 2**20
        ),
    )(outgoing)


def collect(part, experts, owners, pieces):
    capacity, width = part.shape[0] // (experts * owners), part.shape[1] // pieces
    dma = pltpu.SemaphoreType.DMA
    slabs = lambda *lead: pltpu.VMEM(lead + (capacity, width), part.dtype)
    return pl.pallas_call(
        partial(collect_kernel, experts, owners, pieces),
        out_shape=jax.ShapeDtypeStruct((experts, capacity, width), part.dtype),
        in_specs=[pl.BlockSpec(memory_space=pltpu.VMEM)],
        out_specs=pl.BlockSpec(memory_space=pltpu.VMEM),
        scratch_shapes=[
            slabs(pieces, experts, owners),
            slabs(max(owners - 1, 1), pieces, experts),
            slabs(max(pieces - 1, 1), experts),
            slabs(max(pieces - 1, 1), experts),
            slabs(experts),
            dma((2, owners, pieces, experts)),
            dma((2, pieces, experts)),
            dma((2, experts)),
        ],
        compiler_params=pltpu.CompilerParams(
            collective_id=1, has_side_effects=True, vmem_limit_bytes=60 * 2**20
        ),
    )(part)


def per_device(tokens, norm_gain, router_weight, expert_ids, gate_proj, up_proj, down_proj):
    tok_rows, local_width = tokens.shape
    experts = router_weight.shape[1]
    groups, pieces = lax.axis_size("grp"), lax.axis_size("tp")
    owners = groups // experts
    capacity = CAP
    start = lax.axis_index("tp") * local_width
    gain = lax.dynamic_slice_in_dim(norm_gain, start, local_width)
    router = lax.dynamic_slice_in_dim(router_weight, start, local_width, axis=0)
    values = tokens.astype(jnp.float32)
    squares = jnp.sum(values * values, axis=-1)
    squares = jnp.sum(lax.all_gather(squares, "tp"), axis=0)
    mean_square = (squares / (local_width * pieces))[:, None]
    normed = (values * lax.rsqrt(mean_square + epsilon) * gain).astype(jnp.bfloat16)
    logits = jnp.dot(normed, router, preferred_element_type=jnp.float32)
    logits = jnp.sum(lax.all_gather(logits, "tp"), axis=0)
    expert_iota = jnp.arange(experts, dtype=jnp.int32)[None, :]
    chosen_first = (expert_ids[:, 0:1] == expert_iota).astype(jnp.int32)
    chosen_second = (expert_ids[:, 1:2] == expert_iota).astype(jnp.int32)
    first_logit = jnp.sum(logits * chosen_first.astype(jnp.float32), axis=-1)
    second = jnp.sum(logits * chosen_second.astype(jnp.float32), axis=-1)
    gate_first = 1.0 / (1.0 + jnp.exp(second - first_logit))
    gate_second = 1.0 / (1.0 + jnp.exp(first_logit - second))
    gate_table = gate_first[:, None] * chosen_first.astype(jnp.float32) + gate_second[
        :, None
    ] * chosen_second.astype(jnp.float32)
    routed = chosen_first + chosen_second
    slot_index = jnp.cumsum(routed, axis=0) - 1
    slot_iota = jnp.arange(capacity, dtype=jnp.int32)
    slot_picks = (slot_index.T[:, None, :] == slot_iota[None, :, None]) & (
        routed.T[:, None, :] == 1
    )
    selector = slot_picks.astype(jnp.bfloat16)
    outgoing = jnp.einsum(
        "ect,td->ecd", selector, normed, preferred_element_type=jnp.float32
    ).astype(jnp.bfloat16)
    row_block = dispatch(outgoing, owners, pieces)
    gate_act = jnp.dot(row_block, gate_proj, preferred_element_type=jnp.float32)
    up_act = jnp.dot(row_block, up_proj, preferred_element_type=jnp.float32)
    hidden = (jax.nn.silu(gate_act) * up_act).astype(jnp.bfloat16)
    partial_out = jnp.dot(hidden, down_proj, preferred_element_type=jnp.float32).astype(
        jnp.bfloat16
    )
    summed = collect(partial_out, experts, owners, pieces).astype(jnp.float32)
    combine = slot_picks.astype(jnp.float32) * gate_table.T[:, None, :]
    mixed = jnp.einsum("ect,ecd->td", combine, summed, precision=lax.Precision.HIGHEST)
    return mixed.astype(jnp.bfloat16)


def solution(mesh):
    in_specs = (
        P("grp", "tp"),
        P(),
        P(),
        P("grp", None),
        P(None, ("grp", "tp")),
        P(None, ("grp", "tp")),
        P(("grp", "tp"), None),
    )
    out_specs = P("grp", "tp")
    return jax.shard_map(
        per_device, mesh=mesh, in_specs=in_specs, out_specs=out_specs, check_vma=False
    )
```

profile of v0, /device:TPU:13, one launch (start us, length us, event | category | flops | bytes accessed | tf_op | source)
XLA Modules:
  0.0 148.9 jit_solution(2890629006017018905)
XLA Ops:
  0.0 0.0 copy-start
  0.0 1.3 dynamic-slice
  1.9 1.2 fusion.8
  3.1 0.2 dynamic-update-slice
  3.4 3.8 %all-reduce = f32[128]{0:T(128)S(1)} all-reduce(f32[128]{0:T(128)S(1)} %dynamic-update-slice), channel_id=2, replica_groups=mesh['grp'=16,'tp'=2] {'tp'}, use_global_device_ids=true, to_apply=%add | all-reduce | flops 128 | bytes 1024
  7.1 0.1 reshape.131
  7.2 0.8 slice_bitcast_fusion.1
  8.0 0.7 dynamic_slice.6
  8.7 0.0 copy-done
  8.7 1.3 convolution_bitcast_fusion.1
  10.0 3.2 %all-gather.2 = f32[2,64,8]{1,2,0:T(8,128)S(1)} all-gather(f32[1,64,8]{1,2,0:T(8,128)S(1)} %convolution_bitcast_fusion.1), channel_id=3, replica_groups=mesh['grp'=16,'tp'=2] {'tp'}, dimensions={0}, use_global_device_ids=true | all-gather | bytes 6144 | tf_op jit(solution)/shard_map/all_gather | solution.py:226
  13.3 0.1 copy.9
  13.4 0.1 reduce_window_sum.11
  13.5 0.1 copy.10
  13.5 2.5 %convolution_convert_fusion.1.src = bf16[8,18,3072]{2,1,0:T(8,128)(2,1)} fusion(bf16[64,3072]{1,0:T(8,128)(2,1)} %param.7, f32[3072]{0:T(1024)S(1)} %dynamic_slice.6, f32[64]{0:T(128)S(1)} %add_rsqrt_fusion, s32[8,64]{1,0:T(8,128)S(1)} %copy.10, pred[8,64]{1,0:T(8,128)(4,1)S(1)} %fusion.31), kind=kOutput, calls=%fused_computation.1 | convolution fusion | flops 57870336 | bytes 1293056 | tf_op jit(solution)/shard_map/ect,td->ecd/dot_general | solution.py:244
  16.1 44.8 %shard_map.73 = bf16[288,6144]{1,0:T(8,128)(2,1)} custom-call(bf16[8,18,3072]{2,1,0:T(8,128)(2,1)} %convolution_convert_fusion.1.src), custom_call_target="tpu_custom_call" | custom-call | tf_op jit(solution)/shard_map/pallas_call | solution.py:165
  60.9 13.2 %fusion.36 = f32[288,2048]{1,0:T(8,128)S(1)} fusion(bf16[288,6144]{1,0:T(8,128)(2,1)} %shard_map.73, bf16[6144,2048]{1,0:T(8,128)(2,1)} %param.11), kind=kOutput, calls=%fused_computation.56 | convolution fusion | flops 7247757312 | bytes 31064064 | tf_op jit(solution)/shard_map/dot_general | solution.py:248
  74.1 0.0 copy-start.1
  74.1 24.7 %convolution_convert_fusion.rows_in = bf16[288,6144]{1,0:T(8,128)(2,1)} fusion(bf16[2048,6144]{1,0:T(8,128)(2,1)} %param.13, bf16[288,6144]{1,0:T(8,128)(2,1)} %shard_map.73, bf16[6144,2048]{1,0:T(8,128)(2,1)} %param.12, f32[288,2048]{1,0:T(8,128)S(1)} %fusion.36), kind=kOutput, calls=%fused_computation | convolution fusion | flops 14500823040 | bytes 59768832 | tf_op jit(solution)/shard_map/dot_general | solution.py:251
  98.8 47.3 %shard_map.74 = bf16[8,18,3072]{2,1,0:T(8,128)(2,1)} custom-call(bf16[288,6144]{1,0:T(8,128)(2,1)} %convolution_convert_fusion.rows_in), custom_call_target="tpu_custom_call" | custom-call | tf_op jit(solution)/shard_map/pallas_call | solution.py:190
  146.1 2.8 %fusion = bf16[64,3072]{1,0:T(8,128)(2,1)} fusion(bf16[8,18,3072]{2,1,0:T(8,128)(2,1)} %shard_map.74, f32[8,64]{1,0:T(8,128)S(1)} %fusion.30, s32[8,64]{1,0:T(8,128)S(1)} %copy.10, pred[8,64]{1,0:T(8,128)(4,1)S(1)} %fusion.31), kind=kOutput, calls=%fused_computation.3 | convolution fusion | flops 339962880 | bytes 1282560 | tf_op jit(solution)/shard_map/ect,ecd->td/dot_general | solution.py:256
  148.9 0.0 copy-done.1
  (10 shorter events, 0.1 us)
Async XLA Ops:
  0.0 8.7 %copy-start = (bf16[6144,8]{0,1:T(8,128)(2,1)S(1)}, bf16[6144,8]{0,1:T(8,128)(2,1)}, u32[]{:S(2)}) copy-start(bf16[6144,8]{0,1:T(8,128)(2,1)} %param.9) | copy-start | bytes 294916
  74.1 74.8 %copy-start.1 = (bf16[6144,8]{0,1:T(8,128)(2,1)S(1)}, bf16[6144,8]{0,1:T(8,128)(2,1)}, u32[]{:S(2)}) copy-start(bf16[6144,8]{0,1:T(8,128)(2,1)} %param.9) | copy-start | bytes 294916
where the time goes:
time: 149 us
  Pallas kernels  92.1 us (62%)
  matrix products  44.6 us (30%)
  blocking collectives  6.96 us (5%)
  local copies, waits for them, and re-layouts  3.23 us (2%)
    pallas_call x1, Pallas kernels, collect(): pl.pallas_call(partial(collect_kernel, experts, owners, pieces), out_shap...  47.3 us
    pallas_call x1, Pallas kernels, dispatch(): pl.pallas_call(partial(dispatch_kernel, experts, owners, pieces), out_sha...  44.8 us
    dot_general x1, matrix products, per_device(): jnp.dot(hidden, down_proj, preferred_element_type=jnp.float32)  24.7 us
    dot_general x1, matrix products, per_device(): gate_act = jnp.dot(row_block, gate_proj, preferred_element_type=jnp.float32)  13.2 us
    unnamed x1, blocking collectives  3.75 us
    all_gather x1, blocking collectives, per_device(): logits = jnp.sum(lax.all_gather(logits, 'tp'), axis=0)  3.2 us

commit v1 on v0

--- a/solution.py
+++ b/solution.py
@@ -208,12 +208,434 @@
     )(part)
 
 
+TILE = 16
+
+
+def shifted(value, amount):
+    return value >> amount
+
+
+def bits_of(number):
+    return number.bit_length() - 1
+
+
+def unpacking(blocks, extra):
+    segments = TILE // extra
+    size = blocks * TILE
+    row = lax.broadcasted_iota(jnp.int32, (size, size), 0)
+    col = lax.broadcasted_iota(jnp.int32, (size, size), 1)
+    per = blocks * extra
+    row_segment, row_rest = shifted(row, bits_of(per)), row & (per - 1)
+    col_block, col_rest = shifted(col, bits_of(TILE)), col & (TILE - 1)
+    same = (row_segment == shifted(col_rest, bits_of(extra))) & (
+        shifted(row_rest, bits_of(extra)) == col_block
+    )
+    same = same & ((row & (extra - 1)) == (col & (extra - 1)))
+    return row, col, same
+
+
+def one_hot(mask):
+    return jnp.where(mask, 1.0, 0.0).astype(jnp.bfloat16)
+
+
+def mm(a, b):
+    return jnp.dot(a, b, preferred_element_type=jnp.float32)
+
+
+def fused_kernel(
+    experts, capacity, chunks, slots,
+    tokens_in, gain_in, router_in, ids, gate_w, up_w, down_w, out,
+    tokens, gain, router, normed, stats, scores, sel_out, mix, unpack_all, unpack_own, pack_all,
+    outgoing, rows, lhs, gate_acc, up_acc, hidden, ring, rest, part, near, leaving, arrived, final, back,
+    load_s, ring_s, small_s, z_s, x_s, core_s, near_s, leave_s, back_s,
+):
+    g, p = lax.axis_index("grp"), lax.axis_index("tp")
+    c, k = g // 2, lax.rem(g, 2)
+    across, twin = (g, 1 - p), (c * 2 + 1 - k, p)
+    tok, width = tokens.shape
+    cw = width // chunks
+    extra = capacity - TILE
+    segments = TILE // extra
+    segw = cw // segments
+    depth = ring.shape[1]
+    total_rows = 2 * experts * capacity
+    main_rows = 2 * experts * TILE
+    halves = gate_w.shape[1] // ring.shape[2]
+    tiles = 2
+    tile = ring.shape[2] // tiles
+    half_of = lambda own: p if own else 1 - p
+    steps = [(own, ch) for ch in range(chunks) for own in (True, False)]
+    yields = [(own, ch) for ch in range(chunks) for own in (False, True)]
+    per_step = 2 * halves
+    in_units = len(steps) * per_step
+    units = in_units + len(yields) * halves
+
+    def unit(i):
+        if i < in_units:
+            step, kind = divmod(i, per_step)
+            n, which = divmod(kind, 2)
+            own, ch = steps[step]
+            row = pl.multiple_of(half_of(own) * width + ch * cw, cw)
+            src = (gate_w, up_w)[which].at[pl.ds(row, depth), pl.ds(n * ring.shape[2], ring.shape[2])]
+        else:
+            q, n = divmod(i - in_units, halves)
+            own, ch = yields[q]
+            col = pl.multiple_of(half_of(own) * width + ch * cw, cw)
+            src = down_w.at[pl.ds(n * depth, depth), pl.ds(col, cw)]
+        return pltpu.make_async_copy(src, ring.at[i % slots], ring_s.at[i % slots])
+
+    barrier = pltpu.get_barrier_semaphore()
+    peers = [(lax.rem(c + j, experts) * 2 + k, p) for j in range(1, experts)] + [twin, across]
+    for peer in peers:
+        pl.semaphore_signal(barrier, inc=1, device_id=peer, device_id_type=MESH)
+    start = pl.multiple_of(p * width, width)
+    loads = [
+        pltpu.make_async_copy(tokens_in, tokens, load_s.at[0]),
+        pltpu.make_async_copy(gain_in.at[:, pl.ds(start, width)], gain, load_s.at[1]),
+        pltpu.make_async_copy(router_in.at[pl.ds(start, width), :], router, load_s.at[2]),
+    ]
+    for load in loads:
+        load.start()
+    for i in range(slots):
+        unit(i).start()
+
+    lanes = lax.broadcasted_iota(jnp.int32, (tok, 128), 1)
+    chosen_first = jnp.where(ids[:, 0:1] == lanes, 1.0, 0.0)
+    chosen_second = jnp.where(ids[:, 1:2] == lanes, 1.0, 0.0)
+    routed = chosen_first + chosen_second
+    t_row = lax.broadcasted_iota(jnp.int32, (tok, tok), 0)
+    t_col = lax.broadcasted_iota(jnp.int32, (tok, tok), 1)
+    place_of = mm(one_hot(t_col <= t_row), routed.astype(jnp.bfloat16)) * routed
+    wide = 2 * 128
+    e_row = lax.broadcasted_iota(jnp.int32, (128, wide), 0)
+    e_col = lax.broadcasted_iota(jnp.int32, (128, wide), 1)
+    main_cols = experts * TILE
+    over = e_col - main_cols
+    owner = jnp.where(e_col < main_cols, shifted(e_col, bits_of(TILE)), shifted(over, bits_of(extra)))
+    spread = one_hot((owner == e_row) & (e_col < experts * capacity))
+    col = lax.broadcasted_iota(jnp.int32, (tok, wide), 1)
+    wanted = jnp.where(col < main_cols, col & (TILE - 1), TILE + (col & (extra - 1))) + 1
+    match = jnp.where(mm(place_of.astype(jnp.bfloat16), spread) == wanted.astype(jnp.float32), 1.0, 0.0)
+    sel_out[...] = match.T[: experts * capacity].astype(jnp.bfloat16)
+
+    _, _, same = unpacking(experts, extra)
+    unpack_own[...] = one_hot(same)
+    row, colm, same = unpacking(2 * experts, extra)
+    unpack_all[...] = one_hot(same)
+    row2 = lax.broadcasted_iota(jnp.int32, row.shape, 1)
+    col2 = lax.broadcasted_iota(jnp.int32, row.shape, 0)
+    per = 2 * experts * extra
+    same = (shifted(row2, bits_of(per)) == shifted(col2 & (TILE - 1), bits_of(extra))) & (
+        shifted(row2 & (per - 1), bits_of(extra)) == shifted(col2, bits_of(TILE))
+    )
+    pack_all[...] = one_hot(same & ((row2 & (extra - 1)) == (col2 & (extra - 1))))
+
+    loads[0].wait()
+    squares = jnp.zeros((tok, 128), jnp.float32)
+    for i in range(width // 128):
+        v = tokens[:, i * 128 : (i + 1) * 128].astype(jnp.float32)
+        squares = squares + v * v
+    stats[0] = squares
+    pl.semaphore_wait(barrier, len(peers))
+    stat_copy = remote(stats.at[0], stats.at[1], small_s, (0,), across)
+    stat_copy.start()
+    loads[1].wait()
+    stat_copy.wait_recv()
+    mean_square = jnp.sum(stats[0] + stats[1], axis=1, keepdims=True) / (2 * width)
+    inverse = lax.rsqrt(mean_square + epsilon)
+
+    def sends(ch, j):
+        e = lax.rem(c + j, experts)
+        return remote(outgoing.at[ch, e], rows.at[p, ch, k, c], z_s, (ch, j), (e * 2 + k, p))
+
+    def forwards(ch, j):
+        slab = rows.at[p, ch, k, lax.rem(c + experts - j, experts)]
+        return remote(slab, slab, x_s, (ch, j), across)
+
+    for ch in range(chunks):
+        span = slice(ch * cw, (ch + 1) * cw)
+        values = tokens[:, span].astype(jnp.float32)
+        normed_now = (values * inverse * gain[:, span]).astype(jnp.bfloat16)
+        normed[:, span] = normed_now
+        picked = mm(sel_out[...], normed_now).astype(jnp.bfloat16)
+        outgoing[ch, :, :, 0:cw] = picked[:main_cols].reshape(experts, TILE, cw)
+        over_rows = picked[main_cols:]
+        stacked = jnp.concatenate([over_rows[:, s * segw : (s + 1) * segw] for s in range(segments)], axis=0)
+        r8 = lax.broadcasted_iota(jnp.int32, (main_cols, main_cols), 1)
+        c8 = lax.broadcasted_iota(jnp.int32, (main_cols, main_cols), 0)
+        per8 = experts * extra
+        same8 = (shifted(r8, bits_of(per8)) == shifted(c8 & (TILE - 1), bits_of(extra))) & (
+            shifted(r8 & (per8 - 1), bits_of(extra)) == shifted(c8, bits_of(TILE))
+        )
+        pack_own = one_hot(same8 & ((r8 & (extra - 1)) == (c8 & (extra - 1))))
+        packed = mm(pack_own, stacked).astype(jnp.bfloat16)
+        outgoing[ch, :, :, cw:] = packed.reshape(experts, TILE, segw)
+        for j in range(1, experts):
+            sends(ch, j).start()
+        rows[p, ch, k, c] = outgoing[ch, c]
+        forwards(ch, 0).start()
+
+    loads[2].wait()
+    scores[0] = jnp.zeros((tok, 128), jnp.float32)
+    scores[0, :, 0:experts] = mm(normed[...], router[...])
+    score_copy = remote(scores.at[0], scores.at[1], small_s, (1,), across)
+    score_copy.start()
+
+    def z_step(ch, j):
+        sends(ch, j).wait_recv()
+        forwards(ch, j).start()
+
+    def twins(own, ch):
+        block = rows.at[half_of(own), ch, k]
+        return remote(block, block, core_s, (0 if own else 1, ch), twin)
+
+    def to_twin(own, ch):
+        twins(own, ch).start()
+
+    def x_wait(ch):
+        for j in range(experts):
+            forwards(ch, j).wait_recv()
+        to_twin(False, ch)
+
+    def gather_rows(own, ch):
+        h = half_of(own)
+        twins(own, ch).wait_recv()
+        lhs[0:main_rows] = rows[h, ch, :, :, :, 0:cw].reshape(main_rows, cw)
+        packed = rows[h, ch, :, :, :, cw:].reshape(main_rows, segw)
+        loose = mm(unpack_all[...], packed).astype(jnp.bfloat16)
+        per = 2 * experts * extra
+        lhs[main_rows:] = jnp.concatenate([loose[s * per : (s + 1) * per] for s in range(segments)], axis=1)
+
+    def step(index, hooks):
+        own, ch = steps[index]
+        gather_rows(own, ch)
+        first, last = index == 0, index == len(steps) - 1
+
+        def body(it, carry):
+            for at, hook in hooks.items():
+                pl.when(it == at)(hook)
+            n = it // tiles
+            base = index * per_step + 2 * n
+            slot_g, slot_u = lax.rem(base, slots), lax.rem(base + 1, slots)
+
+            @pl.when(lax.rem(it, tiles) == 0)
+            def _():
+                src = gate_w.at[pl.ds(0, depth), pl.ds(0, ring.shape[2])]
+                pltpu.make_async_copy(src, ring.at[slot_g], ring_s.at[slot_g]).wait()
+                pltpu.make_async_copy(src, ring.at[slot_u], ring_s.at[slot_u]).wait()
+
+            inner = pl.ds(pl.multiple_of(lax.rem(it, tiles) * tile, tile), tile)
+            outer = pl.ds(pl.multiple_of(it * tile, tile), tile)
+            x = lhs[...]
+            gate = mm(x, ring[slot_g, :, inner])
+            up = mm(x, ring[slot_u, :, inner])
+            if not first:
+                gate = gate + gate_acc[:, outer]
+                up = up + up_acc[:, outer]
+            if last:
+                hidden[:, outer] = (gate / (1.0 + jnp.exp(-gate)) * up).astype(jnp.bfloat16)
+            else:
+                gate_acc[:, outer] = gate
+                up_acc[:, outer] = up
+            return carry
+
+        lax.fori_loop(0, halves * tiles, body, 0)
+        for i in range(slots + index * per_step, min(slots + (index + 1) * per_step, units)):
+            unit(i).start()
+
+    for j in range(1, experts):
+        z_step(0, j)
+    to_twin(True, 0)
+    for ch in range(chunks):
+        if ch + 1 < chunks:
+            nxt = ch + 1
+            z_step(nxt, 1)
+            step(2 * ch, {i: partial(z_step, nxt, 2 + i) for i in range(4)})
+            x_wait(ch)
+            z_step(nxt, 6)
+            z_step(nxt, 7)
+            to_twin(True, nxt)
+            step(2 * ch + 1, {})
+        else:
+            step(2 * ch, {2: partial(x_wait, ch)})
+            step(2 * ch + 1, {})
+
+    score_copy.wait_recv()
+    logits = scores[0] + scores[1]
+    first_logit = jnp.sum(logits * chosen_first, axis=1, keepdims=True)
+    second_logit = jnp.sum(logits * chosen_second, axis=1, keepdims=True)
+    gate_first = 1.0 / (1.0 + jnp.exp(second_logit - first_logit))
+    gate_second = 1.0 / (1.0 + jnp.exp(first_logit - second_logit))
+    table = gate_first * chosen_first + gate_second * chosen_second
+    high = table.astype(jnp.bfloat16)
+    low = (table - high.astype(jnp.float32)).astype(jnp.bfloat16)
+    kept = experts * capacity
+    mix[0:tok] = (mm(high, spread) * match)[:, :kept].astype(jnp.bfloat16)
+    mix[tok:] = (mm(low, spread) * match)[:, :kept].astype(jnp.bfloat16)
+
+    nears, leaves, backs = {}, {}, {}
+
+    def produce(q):
+        base = in_units + q * halves
+
+        def body(it, carry):
+            inner = pl.ds(pl.multiple_of(it * tile, tile), tile)
+            result = None
+            for n in range(halves):
+                slot = (base + n) % slots
+                if True:
+
+                    @pl.when(it == 0)
+                    def _():
+                        unit(base + n).wait()
+
+            for n in range(halves):
+                slot = (base + n) % slots
+                piece = mm(hidden[:, n * depth : (n + 1) * depth], ring[slot, :, inner])
+                result = piece if result is None else result + piece
+            result = result.astype(jnp.bfloat16)
+            part[q, :, :, :, inner] = result[:main_rows].reshape(2, experts, TILE, tile)
+            rest[:, inner] = result[main_rows:]
+            return carry
+
+        lax.fori_loop(0, tiles, body, 0)
+        stacked = jnp.concatenate([rest[:, s * segw : (s + 1) * segw] for s in range(segments)], axis=0)
+        packed = mm(pack_all[...], stacked).astype(jnp.bfloat16)
+        part[q, :, :, :, cw:] = packed.reshape(2, experts, TILE, segw)
+        nears[q] = remote(part.at[q, 1 - k], near.at[q], near_s, (q,), twin)
+        nears[q].start()
+
+    def leave(ch):
+        q = 2 * ch
+        nears[q].wait_recv()
+        for j in list(range(1, experts)) + [0]:
+            s = lax.rem(c + j, experts)
+            both = part[q, k, s].astype(jnp.float32) + near[q, s].astype(jnp.float32)
+            leaving[ch, j] = both.astype(jnp.bfloat16)
+            leaves[ch, j] = remote(leaving.at[ch, j], arrived.at[ch, j], leave_s, (ch, j), across)
+            leaves[ch, j].start()
+
+    def give(ch, j):
+        q = 2 * ch + 1
+        s = lax.rem(c + j, experts)
+        leaves[ch, j].wait_recv()
+        both = part[q, k, s].astype(jnp.float32) + near[q, s].astype(jnp.float32)
+        both = (both + arrived[ch, j].astype(jnp.float32)).astype(jnp.bfloat16)
+        if j == 0:
+            back[ch, c] = both
+        else:
+            final[ch, j] = both
+            backs[ch, j] = remote(final.at[ch, j], back.at[ch, c], back_s, (ch, j), (s * 2 + k, p))
+            backs[ch, j].start()
+
+    def combine(ch):
+        for j in range(1, experts):
+            backs[ch, j].wait_recv()
+        main = back[ch, :, :, 0:cw].reshape(main_cols, cw)
+        packed = back[ch, :, :, cw:].reshape(main_cols, segw)
+        loose = mm(unpack_own[...], packed).astype(jnp.bfloat16)
+        per = experts * extra
+        loose = jnp.concatenate([loose[s * per : (s + 1) * per] for s in range(segments)], axis=1)
+        both = mm(mix[...], jnp.concatenate([main, loose], axis=0))
+        out[:, ch * cw : (ch + 1) * cw] = (both[:tok] + both[tok:]).astype(out.dtype)
+
+    produce(0)
+    produce(1)
+    leave(0)
+    nears[1].wait_recv()
+    for ch in range(1, chunks):
+        produce(2 * ch)
+        produce(2 * ch + 1)
+        leave(ch)
+        nears[2 * ch + 1].wait_recv()
+        if ch == 1:
+            for j in (1, 2):
+                give(0, j)
+    for ch in range(chunks):
+        for j in list(range(1 if ch else 3, experts)) + [0]:
+            give(ch, j)
+        if ch:
+            combine(ch - 1)
+    combine(chunks - 1)
+    for ch in range(chunks):
+        for j in range(experts):
+            if j:
+                sends(ch, j).wait_send()
+            forwards(ch, j).wait_send()
+        twins(True, ch).wait_send()
+        twins(False, ch).wait_send()
+    for copies in (nears, leaves, backs):
+        for copy in copies.values():
+            copy.wait_send()
+    stat_copy.wait_send()
+    score_copy.wait_send()
+
+
+def fused(tokens, norm_gain, router_weight, expert_ids, gate_proj, up_proj, down_proj, chunks):
+    tok, width = tokens.shape
+    experts, capacity, slots = router_weight.shape[1], CAP, 18
+    cw = width // chunks
+    extra = capacity - TILE
+    segw = cw * extra // TILE
+    sw = cw + segw
+    local = gate_proj.shape[1]
+    total = 2 * experts * capacity
+    kept = experts * capacity
+    dma = pltpu.SemaphoreType.DMA
+    bf = lambda *shape: pltpu.VMEM(shape, jnp.bfloat16)
+    fl = lambda *shape: pltpu.VMEM(shape, jnp.float32)
+    anywhere = pl.BlockSpec(memory_space=pl.ANY)
+    inside = pl.BlockSpec(memory_space=pltpu.VMEM)
+    return pl.pallas_call(
+        partial(fused_kernel, experts, capacity, chunks, slots),
+        out_shape=jax.ShapeDtypeStruct((tok, width), jnp.bfloat16),
+        in_specs=[anywhere, anywhere, anywhere, inside, anywhere, anywhere, anywhere],
+        out_specs=inside,
+        scratch_shapes=[
+            bf(tok, width), fl(1, width), bf(width, experts), bf(tok, width),
+            fl(2, tok, 128), fl(2, tok, 128), bf(kept, tok), bf(2 * tok, kept),
+            bf(2 * experts * TILE, 2 * experts * TILE), bf(experts * TILE, experts * TILE),
+            bf(2 * experts * TILE, 2 * experts * TILE),
+            bf(chunks, experts, TILE, sw),
+            bf(2, chunks, 2, experts, TILE, sw),
+            bf(total, cw), fl(total, local), fl(total, local), bf(total, local),
+            bf(slots, cw, cw),
+            bf(2 * experts * extra, cw),
+            bf(2 * chunks, 2, experts, TILE, sw),
+            bf(2 * chunks, experts, TILE, sw),
+            bf(chunks, experts, TILE, sw), bf(chunks, experts, TILE, sw),
+            bf(chunks, experts, TILE, sw), bf(chunks, experts, TILE, sw),
+            dma((3,)), dma((slots,)), dma((2, 2)),
+            dma((2, chunks, experts)), dma((2, chunks, experts)), dma((2, 2, chunks)),
+            dma((2, 2 * chunks)), dma((2, chunks, experts)), dma((2, chunks, experts)),
+        ],
+        compiler_params=pltpu.CompilerParams(
+            collective_id=2, has_side_effects=True, vmem_limit_bytes=67043328
+        ),
+    )(tokens, norm_gain.reshape(1, -1), router_weight, expert_ids, gate_proj, up_proj, down_proj)
+
+
+def fits(width, local, experts, owners, pieces):
+    cw = local // 2
+    extra = CAP - TILE
+    return (
+        owners == 2 and pieces == 2 and experts == 8 and width % cw == 0
+        and 0 < extra and TILE % extra == 0 and cw % (128 * (TILE // extra)) == 0
+    )
+
+
 def per_device(tokens, norm_gain, router_weight, expert_ids, gate_proj, up_proj, down_proj):
     tok_rows, local_width = tokens.shape
     experts = router_weight.shape[1]
     groups, pieces = lax.axis_size("grp"), lax.axis_size("tp")
     owners = groups // experts
     capacity = CAP
+    local = gate_proj.shape[1]
+    if fits(local_width, local, experts, owners, pieces):
+        chunks = local_width // (local // 2)
+        return fused(
+            tokens, norm_gain, router_weight, expert_ids, gate_proj, up_proj, down_proj, chunks
+        )
     start = lax.axis_index("tp") * local_width
     gain = lax.dynamic_slice_in_dim(norm_gain, start, local_width)
     router = lax.dynamic_slice_in_dim(router_weight, start, local_width, axis=0)

time: 149 us -> 98.9 us (0.66)
  matrix products: 44.6 us -> 0 us
  blocking collectives: 6.96 us -> 0 us
  local copies, waits for them, and re-layouts: 3.23 us -> 5.42 us
    dot_general x5 -> x0, matrix products: 44.6 us -> none  [the longest x1 24.7 us: per_device(): jnp.dot(hidden, down_proj, preferred_element_type=jnp.float32)]
    unnamed x7 -> x3, local copies, waits for them, and re-layouts: 1.52 us -> 5.42 us
    unnamed x1 -> x0, blocking collectives: 3.75 us -> none
    all_gather x1 -> x0, blocking collectives: 3.2 us -> none  [per_device(): logits = jnp.sum(lax.all_gather(logits, 'tp'), axis=0)]
    pallas_call x2 -> x1, Pallas kernels: 92.1 us -> 93 us  [fused(): pl.pallas_call(partial(fused_kernel, experts, capacity, chunks, slots), o...]
where the time goes in v1:
time: 98.9 us; the launch traced here: 98.4 us
  Pallas kernels  93 us (94%)
  local copies, waits for them, and re-layouts  5.42 us (5%)
    pallas_call x1, Pallas kernels, fused(): pl.pallas_call(partial(fused_kernel, experts, capacity, chunks, slots), o...  93 us
    unnamed x3, local copies, waits for them, and re-layouts  5.42 us

profile of v1, /device:TPU:13, one launch (start us, length us, event | category | flops | bytes accessed | tf_op | source)
XLA Modules:
  0.0 98.4 jit_solution(15846090225569539596)
XLA Ops:
  0.0 1.4 %copy.9.ids = s32[64,2]{1,0:T(8,128)} copy(s32[64,2]{0,1:T(2,128)} %param.10) | data formatting | bytes 1024 | tf_op args[3]
  1.4 2.3 %copy.8.router_in = bf16[6144,8]{1,0:T(8,128)(2,1)} copy(bf16[6144,8]{0,1:T(8,128)(2,1)} %param.9) | data formatting | bytes 196608 | tf_op args[2]
  3.7 93.0 %shard_map.73 = bf16[64,3072]{1,0:T(8,128)(2,1)} custom-call(bf16[64,3072]{1,0:T(8,128)(2,1)} %tokens_in.1, f32[1,6144]{1,0:T(1,128)} %bitcast.1, bf16[6144,8]{1,0:T(8,128)(2,1)} %copy.8.router_in, s32[64,2]{1,0:T(8,128)} %copy.9.ids, bf16[6144,2048]{1,0:T(8,128)(2,1)} %gate_w.1, bf16[6144,2048]{1,0:T(8,128)(2,1)} %up_w.1, bf16[2048,6144]{1,0:T(8,128)(2,1)} %down_w.1), custom_call_target="tpu_custom_call" | custom-call | tf_op jit(solution)/shard_map/pallas_call | solution.py:589
  96.6 1.8 %copy.11 = bf16[64,3072]{1,0:T(8,128)(2,1)} copy(bf16[64,3072]{1,0:T(8,128)(2,1)} %shard_map.73) | data formatting | bytes 786432

commit v2 on v1

--- a/solution.py
+++ b/solution.py
@@ -243,11 +243,11 @@
 
 
 def fused_kernel(
-    experts, capacity, chunks, slots,
+    experts, capacity, chunks, slots, early,
     tokens_in, gain_in, router_in, ids, gate_w, up_w, down_w, out,
     tokens, gain, router, normed, stats, scores, sel_out, mix, unpack_all, unpack_own, pack_all,
-    outgoing, rows, lhs, gate_acc, up_acc, hidden, ring, rest, part, near, leaving, arrived, final, back,
-    load_s, ring_s, small_s, z_s, x_s, core_s, near_s, leave_s, back_s,
+    outgoing, rows, lhs, gate_acc, up_acc, hidden, ring, rest, part, near, leaving, arrived, final, back, mixed,
+    load_s, ring_s, small_s, z_s, x_s, core_s, near_s, leave_s, back_s, out_s,
 ):
     g, p = lax.axis_index("grp"), lax.axis_index("tp")
     c, k = g // 2, lax.rem(g, 2)
@@ -292,16 +292,14 @@
     loads = [
         pltpu.make_async_copy(tokens_in, tokens, load_s.at[0]),
         pltpu.make_async_copy(gain_in.at[:, pl.ds(start, width)], gain, load_s.at[1]),
-        pltpu.make_async_copy(router_in.at[pl.ds(start, width), :], router, load_s.at[2]),
+        pltpu.make_async_copy(router_in.at[:, pl.ds(start, width)], router, load_s.at[2]),
     ]
     for load in loads:
         load.start()
-    for i in range(slots):
-        unit(i).start()
-
-    lanes = lax.broadcasted_iota(jnp.int32, (tok, 128), 1)
-    chosen_first = jnp.where(ids[:, 0:1] == lanes, 1.0, 0.0)
-    chosen_second = jnp.where(ids[:, 1:2] == lanes, 1.0, 0.0)
+
+    named = lax.broadcasted_iota(jnp.int32, (128, tok), 0)
+    chosen_first = jnp.where(ids[0:1, :] == named, 1.0, 0.0).T
+    chosen_second = jnp.where(ids[1:2, :] == named, 1.0, 0.0).T
     routed = chosen_first + chosen_second
     t_row = lax.broadcasted_iota(jnp.int32, (tok, tok), 0)
     t_col = lax.broadcasted_iota(jnp.int32, (tok, tok), 1)
@@ -331,6 +329,8 @@
     pack_all[...] = one_hot(same & ((row2 & (extra - 1)) == (col2 & (extra - 1))))
 
     loads[0].wait()
+    for i in range(early):
+        unit(i).start()
     squares = jnp.zeros((tok, 128), jnp.float32)
     for i in range(width // 128):
         v = tokens[:, i * 128 : (i + 1) * 128].astype(jnp.float32)
@@ -347,6 +347,10 @@
     def sends(ch, j):
         e = lax.rem(c + j, experts)
         return remote(outgoing.at[ch, e], rows.at[p, ch, k, c], z_s, (ch, j), (e * 2 + k, p))
+
+    def send_all(ch):
+        for j in range(1, experts):
+            sends(ch, j).start()
 
     def forwards(ch, j):
         slab = rows.at[p, ch, k, lax.rem(c + experts - j, experts)]
@@ -370,14 +374,18 @@
         pack_own = one_hot(same8 & ((r8 & (extra - 1)) == (c8 & (extra - 1))))
         packed = mm(pack_own, stacked).astype(jnp.bfloat16)
         outgoing[ch, :, :, cw:] = packed.reshape(experts, TILE, segw)
-        for j in range(1, experts):
-            sends(ch, j).start()
+        if ch == 0:
+            send_all(0)
         rows[p, ch, k, c] = outgoing[ch, c]
         forwards(ch, 0).start()
+    for i in range(early, slots):
+        unit(i).start()
 
     loads[2].wait()
     scores[0] = jnp.zeros((tok, 128), jnp.float32)
-    scores[0, :, 0:experts] = mm(normed[...], router[...])
+    scores[0, :, 0:experts] = lax.dot_general(
+        normed[...], router[...], (((1,), (1,)), ((), ())), preferred_element_type=jnp.float32
+    )
     score_copy = remote(scores.at[0], scores.at[1], small_s, (1,), across)
     score_copy.start()
 
@@ -411,24 +419,19 @@
         gather_rows(own, ch)
         first, last = index == 0, index == len(steps) - 1
 
-        def body(it, carry):
-            for at, hook in hooks.items():
-                pl.when(it == at)(hook)
-            n = it // tiles
+        for it in range(halves * tiles):
+            if it in hooks:
+                hooks[it]()
+            n, part_of = divmod(it, tiles)
             base = index * per_step + 2 * n
-            slot_g, slot_u = lax.rem(base, slots), lax.rem(base + 1, slots)
-
-            @pl.when(lax.rem(it, tiles) == 0)
-            def _():
-                src = gate_w.at[pl.ds(0, depth), pl.ds(0, ring.shape[2])]
-                pltpu.make_async_copy(src, ring.at[slot_g], ring_s.at[slot_g]).wait()
-                pltpu.make_async_copy(src, ring.at[slot_u], ring_s.at[slot_u]).wait()
-
-            inner = pl.ds(pl.multiple_of(lax.rem(it, tiles) * tile, tile), tile)
-            outer = pl.ds(pl.multiple_of(it * tile, tile), tile)
+            if part_of == 0:
+                unit(base).wait()
+                unit(base + 1).wait()
+            inner = pl.ds(part_of * tile, tile)
+            outer = pl.ds(it * tile, tile)
             x = lhs[...]
-            gate = mm(x, ring[slot_g, :, inner])
-            up = mm(x, ring[slot_u, :, inner])
+            gate = mm(x, ring[base % slots, :, inner])
+            up = mm(x, ring[(base + 1) % slots, :, inner])
             if not first:
                 gate = gate + gate_acc[:, outer]
                 up = up + up_acc[:, outer]
@@ -437,25 +440,27 @@
             else:
                 gate_acc[:, outer] = gate
                 up_acc[:, outer] = up
-            return carry
-
-        lax.fori_loop(0, halves * tiles, body, 0)
         for i in range(slots + index * per_step, min(slots + (index + 1) * per_step, units)):
             unit(i).start()
 
-    for j in range(1, experts):
-        z_step(0, j)
+    def z_steps(ch, *js):
+        for j in js:
+            z_step(ch, j)
+            if j == 2 and ch + 1 < chunks:
+                send_all(ch + 1)
+
+    z_steps(0, *range(1, experts))
     to_twin(True, 0)
     for ch in range(chunks):
         if ch + 1 < chunks:
             nxt = ch + 1
-            z_step(nxt, 1)
-            step(2 * ch, {i: partial(z_step, nxt, 2 + i) for i in range(4)})
+            z_steps(nxt, 1)
+            step(2 * ch, {1: partial(z_steps, nxt, 2), 2: partial(z_steps, nxt, 3), 3: partial(z_steps, nxt, 4)})
             x_wait(ch)
-            z_step(nxt, 6)
-            z_step(nxt, 7)
+            z_steps(nxt, 5)
+            step(2 * ch + 1, {2: partial(z_steps, nxt, 6)})
+            z_steps(nxt, 7)
             to_twin(True, nxt)
-            step(2 * ch + 1, {})
         else:
             step(2 * ch, {2: partial(x_wait, ch)})
             step(2 * ch + 1, {})
@@ -473,32 +478,22 @@
     mix[0:tok] = (mm(high, spread) * match)[:, :kept].astype(jnp.bfloat16)
     mix[tok:] = (mm(low, spread) * match)[:, :kept].astype(jnp.bfloat16)
 
-    nears, leaves, backs = {}, {}, {}
+    nears, leaves, backs, results = {}, {}, {}, []
 
     def produce(q):
         base = in_units + q * halves
 
-        def body(it, carry):
-            inner = pl.ds(pl.multiple_of(it * tile, tile), tile)
+        for n in range(halves):
+            unit(base + n).wait()
+        for it in range(tiles):
+            inner = pl.ds(it * tile, tile)
             result = None
             for n in range(halves):
-                slot = (base + n) % slots
-                if True:
-
-                    @pl.when(it == 0)
-                    def _():
-                        unit(base + n).wait()
-
-            for n in range(halves):
-                slot = (base + n) % slots
-                piece = mm(hidden[:, n * depth : (n + 1) * depth], ring[slot, :, inner])
+                piece = mm(hidden[:, n * depth : (n + 1) * depth], ring[(base + n) % slots, :, inner])
                 result = piece if result is None else result + piece
             result = result.astype(jnp.bfloat16)
             part[q, :, :, :, inner] = result[:main_rows].reshape(2, experts, TILE, tile)
             rest[:, inner] = result[main_rows:]
-            return carry
-
-        lax.fori_loop(0, tiles, body, 0)
         stacked = jnp.concatenate([rest[:, s * segw : (s + 1) * segw] for s in range(segments)], axis=0)
         packed = mm(pack_all[...], stacked).astype(jnp.bfloat16)
         part[q, :, :, :, cw:] = packed.reshape(2, experts, TILE, segw)
@@ -537,26 +532,30 @@
         per = experts * extra
         loose = jnp.concatenate([loose[s * per : (s + 1) * per] for s in range(segments)], axis=1)
         both = mm(mix[...], jnp.concatenate([main, loose], axis=0))
-        out[:, ch * cw : (ch + 1) * cw] = (both[:tok] + both[tok:]).astype(out.dtype)
+        span = slice(ch * cw, (ch + 1) * cw)
+        mixed[:, span] = (both[:tok] + both[tok:]).astype(out.dtype)
+        results.append(pltpu.make_async_copy(mixed.at[:, span], out.at[:, span], out_s.at[ch]))
+        results[-1].start()
+
+    def gives(ch, *js):
+        if js[0] == 1:
+            nears[2 * ch + 1].wait_recv()
+        for j in js:
+            give(ch, j)
 
     produce(0)
     produce(1)
     leave(0)
-    nears[1].wait_recv()
-    for ch in range(1, chunks):
-        produce(2 * ch)
-        produce(2 * ch + 1)
-        leave(ch)
-        nears[2 * ch + 1].wait_recv()
-        if ch == 1:
-            for j in (1, 2):
-                give(0, j)
-    for ch in range(chunks):
-        for j in list(range(1 if ch else 3, experts)) + [0]:
-            give(ch, j)
-        if ch:
-            combine(ch - 1)
-    combine(chunks - 1)
+    produce(2)
+    gives(0, 1)
+    produce(3)
+    leave(1)
+    gives(0, 2, 3)
+    produce(4)
+    gives(0, 4, 5)
+    produce(5)
+    leave(2)
+    gives(0, 6, 7, 0)
     for ch in range(chunks):
         for j in range(experts):
             if j:
@@ -564,16 +563,25 @@
             forwards(ch, j).wait_send()
         twins(True, ch).wait_send()
         twins(False, ch).wait_send()
-    for copies in (nears, leaves, backs):
-        for copy in copies.values():
-            copy.wait_send()
     stat_copy.wait_send()
     score_copy.wait_send()
+    for ch in range(1, chunks):
+        gives(ch, *range(1, experts), 0)
+        if ch < chunks - 1:
+            combine(ch - 1)
+    for copy in list(nears.values()) + list(leaves.values()):
+        copy.wait_send()
+    for ch in range(chunks - 2, chunks):
+        combine(ch)
+    for copy in backs.values():
+        copy.wait_send()
+    for copy in results:
+        copy.wait()
 
 
 def fused(tokens, norm_gain, router_weight, expert_ids, gate_proj, up_proj, down_proj, chunks):
     tok, width = tokens.shape
-    experts, capacity, slots = router_weight.shape[1], CAP, 18
+    experts, capacity, slots = router_weight.shape[1], CAP, 16
     cw = width // chunks
     extra = capacity - TILE
     segw = cw * extra // TILE
@@ -587,12 +595,12 @@
     anywhere = pl.BlockSpec(memory_space=pl.ANY)
     inside = pl.BlockSpec(memory_space=pltpu.VMEM)
     return pl.pallas_call(
-        partial(fused_kernel, experts, capacity, chunks, slots),
+        partial(fused_kernel, experts, capacity, chunks, slots, slots // 3),
         out_shape=jax.ShapeDtypeStruct((tok, width), jnp.bfloat16),
         in_specs=[anywhere, anywhere, anywhere, inside, anywhere, anywhere, anywhere],
-        out_specs=inside,
+        out_specs=anywhere,
         scratch_shapes=[
-            bf(tok, width), fl(1, width), bf(width, experts), bf(tok, width),
+            bf(tok, width), fl(1, width), bf(experts, width), bf(tok, width),
             fl(2, tok, 128), fl(2, tok, 128), bf(kept, tok), bf(2 * tok, kept),
             bf(2 * experts * TILE, 2 * experts * TILE), bf(experts * TILE, experts * TILE),
             bf(2 * experts * TILE, 2 * experts * TILE),
@@ -604,15 +612,15 @@
             bf(2 * chunks, 2, experts, TILE, sw),
             bf(2 * chunks, experts, TILE, sw),
             bf(chunks, experts, TILE, sw), bf(chunks, experts, TILE, sw),
-            bf(chunks, experts, TILE, sw), bf(chunks, experts, TILE, sw),
+            bf(chunks, experts, TILE, sw), bf(chunks, experts, TILE, sw), bf(tok, width),
             dma((3,)), dma((slots,)), dma((2, 2)),
             dma((2, chunks, experts)), dma((2, chunks, experts)), dma((2, 2, chunks)),
-            dma((2, 2 * chunks)), dma((2, chunks, experts)), dma((2, chunks, experts)),
+            dma((2, 2 * chunks)), dma((2, chunks, experts)), dma((2, chunks, experts)), dma((chunks,)),
         ],
         compiler_params=pltpu.CompilerParams(
             collective_id=2, has_side_effects=True, vmem_limit_bytes=67043328
         ),
-    )(tokens, norm_gain.reshape(1, -1), router_weight, expert_ids, gate_proj, up_proj, down_proj)
+    )(tokens, norm_gain.reshape(1, -1), router_weight.T, expert_ids.T, gate_proj, up_proj, down_proj)
 
 
 def fits(width, local, experts, owners, pieces):

time: 98.9 us -> 79.6 us (0.80)
  Pallas kernels: 93 us -> 77.7 us
  local copies, waits for them, and re-layouts: 5.42 us -> 1.77 us
    pallas_call x1, Pallas kernels: 93 us -> 77.7 us  [fused(): pl.pallas_call(partial(fused_kernel, experts, capacity, chunks, slots, sl...]
    unnamed x3 -> x1, local copies, waits for them, and re-layouts: 5.42 us -> 1.77 us
where the time goes in v2:
time: 79.6 us; the launch traced here: 79.5 us
  Pallas kernels  77.7 us (98%)
  local copies, waits for them, and re-layouts  1.77 us (2%)
    pallas_call x1, Pallas kernels, fused(): pl.pallas_call(partial(fused_kernel, experts, capacity, chunks, slots, sl...  77.7 us
    unnamed x1, local copies, waits for them, and re-layouts  1.77 us

profile of v2, /device:TPU:13, one launch (start us, length us, event | category | flops | bytes accessed | tf_op | source)
XLA Modules:
  0.0 79.5 jit_solution(14620363726237549707)
XLA Ops:
  0.0 77.7 %shard_map.73 = bf16[64,3072]{1,0:T(8,128)(2,1)} custom-call(bf16[64,3072]{1,0:T(8,128)(2,1)} %tokens_in.1, f32[1,6144]{1,0:T(1,128)} %bitcast.4, bf16[8,6144]{1,0:T(8,128)(2,1)} %bitcast.3, s32[2,64]{1,0:T(2,128)} %bitcast.5, bf16[6144,2048]{1,0:T(8,128)(2,1)} %gate_w.1, bf16[6144,2048]{1,0:T(8,128)(2,1)} %up_w.1, bf16[2048,6144]{1,0:T(8,128)(2,1)} %down_w.1), custom_call_target="tpu_custom_call" | custom-call | tf_op jit(solution)/shard_map/pallas_call | solution.py:597
  77.7 1.8 %copy.9 = bf16[64,3072]{1,0:T(8,128)(2,1)} copy(bf16[64,3072]{1,0:T(8,128)(2,1)} %shard_map.73) | data formatting | bytes 786432

commit v3 on v2

--- a/solution.py
+++ b/solution.py
@@ -243,7 +243,7 @@
 
 
 def fused_kernel(
-    experts, capacity, chunks, slots, early,
+    experts, capacity, chunks, slots,
     tokens_in, gain_in, router_in, ids, gate_w, up_w, down_w, out,
     tokens, gain, router, normed, stats, scores, sel_out, mix, unpack_all, unpack_own, pack_all,
     outgoing, rows, lhs, gate_acc, up_acc, hidden, ring, rest, part, near, leaving, arrived, final, back, mixed,
@@ -284,6 +284,14 @@
             src = down_w.at[pl.ds(n * depth, depth), pl.ds(col, cw)]
         return pltpu.make_async_copy(src, ring.at[i % slots], ring_s.at[i % slots])
 
+    issued, used = [0], [0]
+
+    def pump(count):
+        for _ in range(count):
+            if issued[0] < min(units, used[0] + slots):
+                unit(issued[0]).start()
+                issued[0] += 1
+
     barrier = pltpu.get_barrier_semaphore()
     peers = [(lax.rem(c + j, experts) * 2 + k, p) for j in range(1, experts)] + [twin, across]
     for peer in peers:
@@ -329,8 +337,6 @@
     pack_all[...] = one_hot(same & ((row2 & (extra - 1)) == (col2 & (extra - 1))))
 
     loads[0].wait()
-    for i in range(early):
-        unit(i).start()
     squares = jnp.zeros((tok, 128), jnp.float32)
     for i in range(width // 128):
         v = tokens[:, i * 128 : (i + 1) * 128].astype(jnp.float32)
@@ -339,6 +345,7 @@
     pl.semaphore_wait(barrier, len(peers))
     stat_copy = remote(stats.at[0], stats.at[1], small_s, (0,), across)
     stat_copy.start()
+    pump(1)
     loads[1].wait()
     stat_copy.wait_recv()
     mean_square = jnp.sum(stats[0] + stats[1], axis=1, keepdims=True) / (2 * width)
@@ -378,8 +385,7 @@
             send_all(0)
         rows[p, ch, k, c] = outgoing[ch, c]
         forwards(ch, 0).start()
-    for i in range(early, slots):
-        unit(i).start()
+        pump(1)
 
     loads[2].wait()
     scores[0] = jnp.zeros((tok, 128), jnp.float32)
@@ -422,6 +428,7 @@
         for it in range(halves * tiles):
             if it in hooks:
                 hooks[it]()
+            pump(1)
             n, part_of = divmod(it, tiles)
             base = index * per_step + 2 * n
             if part_of == 0:
@@ -440,12 +447,13 @@
             else:
                 gate_acc[:, outer] = gate
                 up_acc[:, outer] = up
-        for i in range(slots + index * per_step, min(slots + (index + 1) * per_step, units)):
-            unit(i).start()
+            if part_of == tiles - 1:
+                used[0] += 2
 
     def z_steps(ch, *js):
         for j in js:
             z_step(ch, j)
+            pump(1)
             if j == 2 and ch + 1 < chunks:
                 send_all(ch + 1)
 
@@ -454,13 +462,23 @@
     for ch in range(chunks):
         if ch + 1 < chunks:
             nxt = ch + 1
-            z_steps(nxt, 1)
-            step(2 * ch, {1: partial(z_steps, nxt, 2), 2: partial(z_steps, nxt, 3), 3: partial(z_steps, nxt, 4)})
-            x_wait(ch)
-            z_steps(nxt, 5)
-            step(2 * ch + 1, {2: partial(z_steps, nxt, 6)})
-            z_steps(nxt, 7)
-            to_twin(True, nxt)
+            step(
+                2 * ch,
+                {
+                    0: partial(z_steps, nxt, 1),
+                    1: partial(z_steps, nxt, 2),
+                    2: lambda: (x_wait(ch), z_steps(nxt, 3)),
+                    3: partial(z_steps, nxt, 4),
+                },
+            )
+            step(
+                2 * ch + 1,
+                {
+                    0: partial(z_steps, nxt, 5),
+                    1: partial(z_steps, nxt, 6),
+                    2: lambda: (z_steps(nxt, 7), to_twin(True, nxt)),
+                },
+            )
         else:
             step(2 * ch, {2: partial(x_wait, ch)})
             step(2 * ch + 1, {})
@@ -494,6 +512,8 @@
             result = result.astype(jnp.bfloat16)
             part[q, :, :, :, inner] = result[:main_rows].reshape(2, experts, TILE, tile)
             rest[:, inner] = result[main_rows:]
+            pump(1)
+        used[0] += halves
         stacked = jnp.concatenate([rest[:, s * segw : (s + 1) * segw] for s in range(segments)], axis=0)
         packed = mm(pack_all[...], stacked).astype(jnp.bfloat16)
         part[q, :, :, :, cw:] = packed.reshape(2, experts, TILE, segw)
@@ -595,7 +615,7 @@
     anywhere = pl.BlockSpec(memory_space=pl.ANY)
     inside = pl.BlockSpec(memory_space=pltpu.VMEM)
     return pl.pallas_call(
-        partial(fused_kernel, experts, capacity, chunks, slots, slots // 3),
+        partial(fused_kernel, experts, capacity, chunks, slots),
         out_shape=jax.ShapeDtypeStruct((tok, width), jnp.bfloat16),
         in_specs=[anywhere, anywhere, anywhere, inside, anywhere, anywhere, anywhere],
         out_specs=anywhere,

time: 79.6 us -> 75 us (0.942)
  Pallas kernels: 77.7 us -> 73 us
    pallas_call x1, Pallas kernels: 77.7 us -> 73 us  [fused(): pl.pallas_call(partial(fused_kernel, experts, capacity, chunks, slots), o...]
where the time goes in v3:
time: 75 us; the launch traced here: 74.8 us
  Pallas kernels  73 us (97%)
  local copies, waits for them, and re-layouts  1.77 us (2%)
    pallas_call x1, Pallas kernels, fused(): pl.pallas_call(partial(fused_kernel, experts, capacity, chunks, slots), o...  73 us
    unnamed x1, local copies, waits for them, and re-layouts  1.77 us

profile of v3, /device:TPU:13, one launch (start us, length us, event | category | flops | bytes accessed | tf_op | source)
XLA Modules:
  0.0 74.8 jit_solution(12294343026955773298)
XLA Ops:
  0.0 73.0 %shard_map.73 = bf16[64,3072]{1,0:T(8,128)(2,1)} custom-call(bf16[64,3072]{1,0:T(8,128)(2,1)} %tokens_in.1, f32[1,6144]{1,0:T(1,128)} %bitcast.4, bf16[8,6144]{1,0:T(8,128)(2,1)} %bitcast.3, s32[2,64]{1,0:T(2,128)} %bitcast.5, bf16[6144,2048]{1,0:T(8,128)(2,1)} %gate_w.1, bf16[6144,2048]{1,0:T(8,128)(2,1)} %up_w.1, bf16[2048,6144]{1,0:T(8,128)(2,1)} %down_w.1), custom_call_target="tpu_custom_call" | custom-call | tf_op jit(solution)/shard_map/pallas_call | solution.py:617
  73.0 1.8 %copy.9 = bf16[64,3072]{1,0:T(8,128)(2,1)} copy(bf16[64,3072]{1,0:T(8,128)(2,1)} %shard_map.73) | data formatting | bytes 786432
